TPU v7x, 32 devices: a whole 2x2x4 slice. The times are simulated.
32 devices in a mesh: section: 16 (over z, y, core), tensor: 2 (over x).
Axes of the slice: x: 2, y: 2, z: 4, core: 2. Of those that a mesh axis runs over, the one named last changes fastest.
Arguments:
- saved: bfloat16 [16, 16, 64, 8192], P('section', None, 'tensor'), may hold values from -6 to 6
- offsets: int32 [16, 16], P('section'), may hold values from 0 to 15, as said below
Outputs:
- restored: float32 [16, 16, 64, 8192], P('section', None, None, 'tensor')
- block_sums: float32 [16, 16, 8192], P('section', None, 'tensor')
Inputs may be any that keep to these rules, and one draw needn't show every extreme that they name: Each row of offsets is a permutation of 0 to 15.
All inputs are finite; a program needn't handle non-finite values.
Results may differ from a plain program's by a relative error of at most 0.0003.
Values may be sent and summed in bfloat16 or wider, within the bound.
A program may use at most 128 MiB of HBM per device.

v0:
```python
import jax
import jax.numpy as jnp
from jax import lax
from jax.sharding import PartitionSpec as P


def invert(table, count):
    return jnp.zeros((count,), jnp.int32).at[table].set(jnp.arange(count, dtype=jnp.int32))


def body(saved, offsets):
    count = lax.axis_size("section")
    mine = lax.axis_index("section")
    table = offsets[0]
    blocks = saved[0]
    order = invert((mine + table) % count, count)
    outgoing = jnp.take(blocks, order, axis=0)
    split_cols = lax.all_to_all(outgoing, "tensor", split_axis=2, concat_axis=1, tiled=True)
    arrived = lax.all_to_all(split_cols, "section", split_axis=0, concat_axis=0, tiled=True)
    restored = arrived.astype(jnp.float32)
    block_sums = jnp.sum(restored, axis=1)
    return (restored[None], block_sums[None])


def solution(mesh):
    return jax.shard_map(
        body,
        mesh=mesh,
        in_specs=(P("section", None, "tensor", None), P("section", None)),
        out_specs=(P("section", None, None, "tensor"), P("section", None, "tensor")),
        check_vma=False,
    )
```

profile of v0, /device:TPU:1, one launch (start us, length us, event | category | flops | bytes accessed | tf_op | source)
XLA Modules:
  0.0 462.9 jit_solution(6065663858853515315)
XLA Ops:
  0.6 0.7 fusion.1
  1.3 0.6 scatter_custom_fusion
  2.0 8.3 %gather_fusion = bf16[16,32,8192]{2,1,0:T(8,128)(2,1)} fusion(bf16[16,32,8192]{2,1,0:T(8,128)(2,1)} %bitcast.18, s32[1024]{0:T(1024)S(1)} %pad_clamp_fusion), kind=kCustom, calls=%fused_computation | custom fusion | bytes 16777280 | tf_op jit(solution)/shard_map/jit(_take)/gather | solution.py:17
  10.3 7.6 %broadcast_select_fusion = bf16[16,32,8192]{2,1,0:T(8,128)(2,1)} fusion(bf16[16,32,8192]{2,1,0:T(8,128)(2,1)} %gather_fusion, pred[16]{0:T(512)(128)(4,1)S(1)} %compare_and_fusion), kind=kLoop, calls=%fused_computation.4 | loop fusion | flops 4194304 | bytes 16777232 | tf_op jit(solution)/shard_map/jit(_take)/select_n | solution.py:17
  17.9 34.7 %copy.6 = bf16[16,32,8192]{1,0,2:T(8,128)(2,1)} copy(bf16[16,32,8192]{2,1,0:T(8,128)(2,1)} %broadcast_select_fusion) | data formatting | bytes 16777216 | tf_op jit(solution)/shard_map/jit(_take)/select_n | solution.py:17
  52.6 27.6 %reshape.82 = bf16[2,2,1048576]{2,1,0:T(2,128)(2,1)} reshape(bf16[8192,16,32]{2,1,0:T(8,128)(2,1)} %bitcast.15) | data formatting | bytes 16777216
  80.2 103.8 %all_to_all.23 = bf16[2,2,1048576]{2,1,0:T(2,128)(2,1)} all-to-all(bf16[2,2,1048576]{2,1,0:T(2,128)(2,1)} %reshape.82), channel_id=1, replica_groups=mesh['section'=16,'tensor'=2] {'tensor'}, dimensions={0} | all-to-all | bytes 16777216 | tf_op jit(solution)/shard_map/all_to_all | solution.py:18
  184.0 38.0 %reshape.83 = bf16[8192,16,32]{2,1,0:T(8,128)(2,1)} reshape(bf16[2,2,1048576]{2,1,0:T(2,128)(2,1)} %all_to_all.23) | data formatting | bytes 16777216
  222.0 33.7 %copy.7 = bf16[16,2,32,4096]{3,2,1,0:T(8,128)(2,1)} copy(bf16[16,2,32,4096]{2,0,3,1:T(8,128)(2,1)} %bitcast.16) | data formatting | bytes 16777216 | tf_op jit(solution)/shard_map/all_to_all | solution.py:18
  255.8 189.7 %all_to_all.24 = bf16[16,64,4096]{2,1,0:T(8,128)(2,1)S(1)} all-to-all(bf16[16,64,4096]{2,1,0:T(8,128)(2,1)} %bitcast.17), channel_id=1, replica_groups=mesh['section'=16,'tensor'=2] {'section'}, dimensions={0} | all-to-all | bytes 16777216 | tf_op jit(solution)/shard_map/all_to_all | solution.py:19
  445.4 0.0 copy-start
  445.5 3.2 copy-done
  448.7 2.4 convert_reduce_fusion
  451.1 11.8 %convert_bitcast_fusion = f32[1,16,64,4096]{3,2,1,0:T(8,128)} fusion(bf16[16,64,4096]{2,1,0:T(8,128)(2,1)} %copy-done), kind=kLoop, calls=%fused_computation.3 | loop fusion | flops 4194304 | bytes 25165824 | tf_op jit(solution)/shard_map/broadcast_in_dim | solution.py:22
  (4 shorter events, 0.0 us)
Async XLA Ops:
  445.4 3.2 copy-start
where the time goes:
time: 465 us; the launch traced here: 463 us
  blocking collectives  294 us (63%)
  local copies, waits for them, and re-layouts  146 us (31%)
  other arithmetic  22.6 us (5%)
    all_to_all x1, blocking collectives, body(): lax.all_to_all(split_cols, 'section', split_axis=0, concat_axis=0, tiled=...  190 us
    all_to_all x1, blocking collectives, body(): lax.all_to_all(outgoing, 'tensor', split_axis=2, concat_axis=1, tiled=True)  104 us
    unnamed x4, local copies, waits for them, and re-layouts  68.8 us
    select_n x1, local copies, waits for them, and re-layouts, body(): outgoing = jnp.take(blocks, order, axis=0)  34.7 us
    all_to_all x1, local copies, waits for them, and re-layouts, body(): lax.all_to_all(outgoing, 'tensor', split_axis=2, concat_axis=1, tiled=True)  33.7 us
    broadcast_in_dim x1, other arithmetic, body(): return (restored[None], block_sums[None])  11.8 us

commit v1 on v0

--- a/solution.py
+++ b/solution.py
@@ -15,7 +15,12 @@
     blocks = saved[0]
     order = invert((mine + table) % count, count)
     outgoing = jnp.take(blocks, order, axis=0)
-    split_cols = lax.all_to_all(outgoing, "tensor", split_axis=2, concat_axis=1, tiled=True)
+    split_cols = jnp.concatenate(
+        lax.all_to_all(
+            jnp.stack(jnp.split(outgoing, lax.axis_size("tensor"), axis=2)), "tensor", 0, 0
+        ),
+        axis=1,
+    )
     arrived = lax.all_to_all(split_cols, "section", split_axis=0, concat_axis=0, tiled=True)
     restored = arrived.astype(jnp.float32)
     block_sums = jnp.sum(restored, axis=1)

time: 465 us -> 349 us (0.75)
  local copies, waits for them, and re-layouts: 146 us -> 25.2 us
  other arithmetic: 22.6 us -> 28.9 us
    unnamed x4 -> x2, local copies, waits for them, and re-layouts: 68.8 us -> 3.22 us
    select_n x1 -> x0, local copies, waits for them, and re-layouts: 34.7 us -> none  [body(): outgoing = jnp.take(blocks, order, axis=0)]
    all_to_all x1 -> x0, local copies, waits for them, and re-layouts: 33.7 us -> none  [body(): lax.all_to_all(outgoing, 'tensor', split_axis=2, concat_axis=1, tiled=True)]
    reshape x0 -> x1, local copies, waits for them, and re-layouts: none -> 7.89 us  [body(): jnp.concatenate(lax.all_to_all(jnp.stack(jnp.split(outgoing, lax.axis_siz...]
    another operation x0 -> x1, other arithmetic: none -> 6.35 us  [body(): jnp.stack(jnp.split(outgoing, lax.axis_size('tensor'), axis=2))]
    another operation x0 -> x1, local copies, waits for them, and re-layouts: none -> 5.13 us  [body(): jnp.stack(jnp.split(outgoing, lax.axis_size('tensor'), axis=2))]
where the time goes in v1:
time: 349 us; the launch traced here: 348 us
  blocking collectives  293 us (84%)
  other arithmetic  28.9 us (8%)
  local copies, waits for them, and re-layouts  25.2 us (7%)
    all_to_all x1, blocking collectives, body(): lax.all_to_all(split_cols, 'section', split_axis=0, concat_axis=0, tiled=...  190 us
    all_to_all x1, blocking collectives, body(): lax.all_to_all(jnp.stack(jnp.split(outgoing, lax.axis_size('tensor'), axi...  104 us
    broadcast_in_dim x1, other arithmetic, body(): return (restored[None], block_sums[None])  11.8 us
    gather x1, local copies, waits for them, and re-layouts, body(): outgoing = jnp.take(blocks, order, axis=0)  8.32 us
    reshape x1, local copies, waits for them, and re-layouts, body(): jnp.concatenate(lax.all_to_all(jnp.stack(jnp.split(outgoing, lax.axis_siz...  7.89 us
    select_n x2, other arithmetic, body(): outgoing = jnp.take(blocks, order, axis=0)  7.65 us

profile of v1, /device:TPU:1, one launch (start us, length us, event | category | flops | bytes accessed | tf_op | source)
XLA Modules:
  0.0 348.3 jit_solution(569677759240871215)
XLA Ops:
  0.6 0.7 fusion.1
  1.3 0.6 scatter_custom_fusion
  2.0 8.3 %gather_fusion = bf16[16,32,8192]{2,1,0:T(8,128)(2,1)} fusion(bf16[16,32,8192]{2,1,0:T(8,128)(2,1)} %bitcast.17, s32[1024]{0:T(1024)S(1)} %pad_clamp_fusion), kind=kCustom, calls=%fused_computation | custom fusion | bytes 16777280 | tf_op jit(solution)/shard_map/jit(_take)/gather | solution.py:17
  10.3 7.6 %broadcast_select_fusion = bf16[16,32,8192]{2,1,0:T(8,128)(2,1)} fusion(bf16[16,32,8192]{2,1,0:T(8,128)(2,1)} %gather_fusion, pred[16]{0:T(512)(128)(4,1)S(1)} %compare_and_fusion), kind=kLoop, calls=%fused_computation.5 | loop fusion | flops 4194304 | bytes 16777232 | tf_op jit(solution)/shard_map/jit(_take)/select_n | solution.py:17
  17.9 5.1 %slice_bitcast_fusion.1 = (bf16[1,16,32,4096]{3,2,1,0:T(8,128)(2,1)S(1)}, bf16[1,16,32,4096]{3,2,1,0:T(8,128)(2,1)}) fusion(bf16[16,32,8192]{2,1,0:T(8,128)(2,1)} %broadcast_select_fusion), kind=kLoop, calls=%fused_computation.7 | loop fusion | bytes 16777216 | tf_op jit(solution)/shard_map/stack | solution.py:20
  23.1 6.3 %pad_maximum_fusion = bf16[2,16,32,4096]{3,2,1,0:T(8,128)(2,1)} fusion(bf16[1,16,32,4096]{3,2,1,0:T(8,128)(2,1)} %get-tuple-element.3, bf16[1,16,32,4096]{3,2,1,0:T(8,128)(2,1)S(1)} %get-tuple-element.2), kind=kLoop, calls=%fused_computation.4 | loop fusion | flops 4194304 | bytes 16777216 | tf_op jit(solution)/shard_map/stack | solution.py:20
  29.4 103.6 %all_to_all.10 = bf16[2,16,32,4096]{3,2,1,0:T(8,128)(2,1)} all-to-all(bf16[2,16,32,4096]{3,2,1,0:T(8,128)(2,1)} %pad_maximum_fusion), channel_id=1, replica_groups=mesh['section'=16,'tensor'=2] {'tensor'}, dimensions={0} | all-to-all | bytes 16777216 | tf_op jit(solution)/shard_map/all_to_all | solution.py:19
  133.0 7.9 %copy.4 = bf16[16,2,32,4096]{3,2,1,0:T(8,128)(2,1)} copy(bf16[16,2,32,4096]{3,2,0,1:T(8,128)(2,1)} %bitcast.15) | data formatting | bytes 16777216 | tf_op jit(solution)/shard_map/reshape | solution.py:18
  140.9 189.9 %all_to_all.11 = bf16[16,64,4096]{2,1,0:T(8,128)(2,1)S(1)} all-to-all(bf16[16,64,4096]{2,1,0:T(8,128)(2,1)} %bitcast.16), channel_id=1, replica_groups=mesh['section'=16,'tensor'=2] {'section'}, dimensions={0} | all-to-all | bytes 16777216 | tf_op jit(solution)/shard_map/all_to_all | solution.py:24
  330.8 0.0 copy-start
  330.8 3.2 copy-done
  334.0 2.4 convert_reduce_fusion
  336.5 11.8 %convert_bitcast_fusion = f32[1,16,64,4096]{3,2,1,0:T(8,128)} fusion(bf16[16,64,4096]{2,1,0:T(8,128)(2,1)} %copy-done), kind=kLoop, calls=%fused_computation.3 | loop fusion | flops 4194304 | bytes 25165824 | tf_op jit(solution)/shard_map/broadcast_in_dim | solution.py:27
  (4 shorter events, 0.0 us)
Async XLA Ops:
  330.8 3.2 copy-start
